TPU v7x, 512 devices: a whole 4x8x8 slice. The times are simulated.
512 devices in a mesh: seq: 128 (over y, z, core), head: 4 (over x).
Axes of the slice: x: 4, y: 8, z: 8, core: 2. Of those that a mesh axis runs over, the one named last changes fastest.
Arguments:
- seq_inputs: bfloat16 [1, 32768, 4096], P(None, 'seq', 'head'), may hold values from -6 to 6
- gate_inputs: bfloat16 [1, 32768, 4096], P(None, 'seq', 'head'), may hold values from -6 to 6
- projections: bfloat16 [1, 32768, 256], P(None, 'seq'), may hold values from -6 to 6
- step_raw: float32 [1, 32768, 64], P(None, 'seq', 'head'), may hold values from -3 to 3
- step_bias: float32 [64], P('head'), may hold values from -1 to 1
- decay_rate: float32 [64], P('head'), may hold values from 3.0517578e-05 to 8
- conv_feature: float32 [4, 4096], P(None, 'head'), may hold values from -3 to 3
- conv_proj: float32 [4, 256], replicated, may hold values from -3 to 3
- norm_gain: float32 [4096], P('head'), may hold values from 0.25 to 1.75
Outputs:
- mixed_out: bfloat16 [1, 32768, 4096], P(None, 'seq', 'head')
All inputs are finite; a program needn't handle non-finite values.
Results may differ from a plain program's by a relative error of at most 0.0034.
Values may be sent and summed in bfloat16 or wider, within the bound.
No kernel may reach another device: no remote copies, remote signals or barrier semaphores. Data moves between devices by JAX's collectives and lax.ppermute only.
A program may use at most 192 MiB of HBM per device.

v0:
```python
import jax
import jax.numpy as jnp
from jax import lax
from jax.sharding import PartitionSpec as P

HEADS = 64
HEAD_DIM = 64
STRETCH = 256


def from_behind(value, axis, steps):
    count = lax.axis_size(axis)
    leading, last = (max(0, -steps), min(count, count - steps))
    return lax.ppermute(value, axis, [(source, source + steps) for source in range(leading, last)])


def sent_to_all(array, axis):
    count = lax.axis_size(axis)
    return lax.all_to_all(
        jnp.broadcast_to(array[None], (count, *array.shape)), axis, 0, 0, tiled=True
    )


def over_copies(array, axis):
    everything = sent_to_all(array, axis)
    return jnp.sum(everything, axis=0)


def causal_mix(window, weights):
    kernel_len = weights.shape[0]
    length = window.shape[1] - kernel_len + 1
    running = window[:, 0:length].astype(jnp.float32) * weights[0]
    for offset in range(1, kernel_len):
        running = (
            running + window[:, offset : offset + length].astype(jnp.float32) * weights[offset]
        )
    return jax.nn.silu(running).astype(jnp.bfloat16)


def block_local(x_mixed, write_vec, read_vec, step_lead, decay_rate):
    flat_count, span, channels = x_mixed.shape
    head_count = decay_rate.shape[0]
    head_width = channels // head_count
    state_size = write_vec.shape[2]
    group_count = head_count // 2
    scores = jnp.einsum("btn,bsn->bts", read_vec, write_vec, preferred_element_type=jnp.float32)
    causal = jnp.arange(span)[:, None] >= jnp.arange(span)[None, :]
    log_lead = jnp.cumsum(step_lead * (-decay_rate)[None, :, None], axis=2)

    def head_group(operands):
        x_group, step_group, log_group = operands
        decay_gap = jnp.where(
            causal[None, None], log_group[:, :, :, None] - log_group[:, :, None, :], 0.0
        )
        mixing = jnp.where(
            causal[None, None],
            scores[:, None] * jnp.exp(decay_gap) * step_group[:, :, None, :],
            0.0,
        ).astype(jnp.bfloat16)
        x_heads = x_group.reshape(flat_count, span, 2, head_width)
        within = jnp.einsum("bhts,bshp->bthp", mixing, x_heads, preferred_element_type=jnp.float32)
        to_end = jnp.exp(log_group[:, :, -1:] - log_group) * step_group
        to_end = jnp.transpose(to_end, (0, 2, 1))
        weighted = (x_heads.astype(jnp.float32) * to_end[:, :, :, None]).astype(jnp.bfloat16)
        summary = jnp.einsum(
            "bshp,bsn->bhpn", weighted, write_vec, preferred_element_type=jnp.float32
        )
        return (within.reshape(flat_count, span, 2 * head_width), summary)

    x_groups = jnp.transpose(
        x_mixed.reshape(flat_count, span, group_count, 2 * head_width), (2, 0, 1, 3)
    )
    step_groups = jnp.transpose(step_lead.reshape(flat_count, group_count, 2, span), (1, 0, 2, 3))
    log_groups = jnp.transpose(log_lead.reshape(flat_count, group_count, 2, span), (1, 0, 2, 3))
    within, summary = lax.map(head_group, (x_groups, step_groups, log_groups))
    within = jnp.transpose(within, (1, 2, 0, 3)).reshape(flat_count, span, channels)
    summary = jnp.transpose(summary, (1, 0, 2, 3, 4)).reshape(
        flat_count, head_count, head_width, state_size
    )
    return (within, summary, log_lead)


def chain_join(earlier, later):
    return (earlier[0] * later[0], later[0] * earlier[1] + later[1])


def shards(
    seq_inputs,
    gate_inputs,
    projections,
    step_raw,
    step_bias,
    decay_rate,
    conv_feature,
    conv_proj,
    norm_gain,
):
    kernel_len = conv_feature.shape[0]
    batch_rows, local_len, channels = seq_inputs.shape
    head_count = decay_rate.shape[0]
    head_width = channels // head_count
    state_size = projections.shape[2] // 2
    block_count = local_len // STRETCH
    flat_count = batch_rows * block_count
    halo_rows = from_behind(
        (seq_inputs[:, local_len - kernel_len + 1 :], projections[:, local_len - kernel_len + 1 :]),
        "seq",
        1,
    )
    x_mixed = causal_mix(jnp.concatenate([halo_rows[0], seq_inputs], axis=1), conv_feature)
    proj_mixed = causal_mix(jnp.concatenate([halo_rows[1], projections], axis=1), conv_proj)
    write_vec = proj_mixed[:, :, :state_size]
    read_vec = proj_mixed[:, :, state_size:]
    step_size = jax.nn.softplus(step_raw + step_bias)
    step_lead = jnp.transpose(step_size, (0, 2, 1))
    within, summary, log_lead = block_local(x_mixed, write_vec, read_vec, step_lead, decay_rate)
    summary = summary.reshape(batch_rows, block_count, head_count, head_width, state_size)
    block_decay = jnp.exp(log_lead[:, :, -1]).reshape(batch_rows, block_count, head_count)
    decay_acc = jnp.ones((batch_rows, head_count), jnp.float32)
    state_acc = jnp.zeros((batch_rows, head_count, head_width, state_size), jnp.float32)
    decay_list = [decay_acc]
    state_list = [state_acc]
    state_acc = block_decay[:, 0, :, None, None] * state_acc + summary[:, 0]
    decay_acc = decay_acc * block_decay[:, 0]
    prior_decay = jnp.stack(decay_list, axis=1)
    prior_state = jnp.stack(state_list, axis=1)
    seq_count = lax.axis_size("seq")
    flat_state = state_acc.reshape(1, batch_rows, head_count, head_width * state_size)
    spread_decay = jnp.broadcast_to(
        decay_acc[None, :, :, None], (1, batch_rows, head_count, seq_count)
    )
    state_slices = lax.all_to_all(flat_state, "seq", split_axis=3, concat_axis=0, tiled=True)
    decay_slices = lax.all_to_all(spread_decay, "seq", split_axis=3, concat_axis=0, tiled=True)
    inclusive = lax.associative_scan(chain_join, (decay_slices, state_slices), axis=0)
    exclusive = jnp.concatenate([jnp.zeros_like(state_slices[0:1]), inclusive[1][:-1]], axis=0)
    returned = lax.all_to_all(exclusive, "seq", split_axis=0, concat_axis=3, tiled=True)
    entering_state = returned.reshape(batch_rows, head_count, head_width, state_size)
    entering = prior_decay[:, :, :, None, None] * entering_state[:, None] + prior_state
    entering = entering.reshape(flat_count, head_count, head_width, state_size).astype(jnp.bfloat16)
    outside = jnp.einsum("bhpn,btn->bthp", entering, read_vec, preferred_element_type=jnp.float32)
    decay_now = jnp.transpose(jnp.exp(log_lead), (0, 2, 1))
    outside = (outside * decay_now[:, :, :, None]).reshape(flat_count, STRETCH, channels)
    total_out = within + outside
    gated = total_out * jax.nn.silu(gate_inputs.astype(jnp.float32))
    squares = over_copies(jnp.sum(gated * gated, axis=-1), "head")
    scale = lax.rsqrt(squares / (HEADS * HEAD_DIM) + 1.0)
    return (gated * scale[:, :, None] * norm_gain).astype(jnp.bfloat16)


def solution(mesh):
    return jax.shard_map(
        shards,
        mesh=mesh,
        in_specs=(
            P(None, "seq", "head"),
            P(None, "seq", "head"),
            P(None, "seq", None),
            P(None, "seq", "head"),
            P("head"),
            P("head"),
            P(None, "head"),
            P(),
            P("head"),
        ),
        out_specs=P(None, "seq", "head"),
        check_vma=False,
    )
```

profile of v0, /device:TPU:8, one launch (start us, length us, event | category | flops | bytes accessed | tf_op | source)
XLA Modules:
  0.0 187.0 jit_solution(816743650927611163)
XLA Ops:
  0.0 0.7 slice.231
  0.7 1.9 %collective-permute-start = (bf16[1,3,1024]{2,1,0:T(4,128)(2,1)S(1)}, bf16[1,3,1024]{2,1,0:T(4,128)(2,1)S(1)}, u32[]{:S(2)}, u32[]{:S(2)}) collective-permute-start(bf16[1,3,1024]{2,1,0:T(4,128)(2,1)S(1)} %slice.231), channel_id=1, source_target_pairs={{0,4},{4,8},{8,12},{12,16},{16,20},{20,24},{24,28},{28,32},{32,36}... | collective-permute-start | bytes 18440 | tf_op jit(solution)/shard_map/ppermute | solution.py:14
  3.3 4.4 %collective-permute-start.1 = (bf16[1,3,256]{2,1,0:T(4,128)(2,1)S(1)}, bf16[1,3,256]{2,1,0:T(4,128)(2,1)S(1)}, u32[]{:S(2)}, u32[]{:S(2)}) collective-permute-start(bf16[1,3,256]{2,1,0:T(4,128)(2,1)S(1)} %slice.239), channel_id=1, source_target_pairs={{0,4},{4,8},{8,12},{12,16},{16,20},{20,24},{24,28},{28,32},{32,36}... | collective-permute-start | bytes 4616 | tf_op jit(solution)/shard_map/ppermute | solution.py:14
  8.4 0.8 multiply_bitcast_fusion
  11.2 16.5 %all-to-all-start.1 = ((f32[1,1,16,128]{2,1,0,3:T(1,128)}), f32[1,1,16,128]{2,1,0,3:T(1,128)S(1)}, u32[]{:S(2)}, u32[]{:S(2)}) async-start(f32[1,1,16,128]{2,1,0,3:T(1,128)} %broadcast_in_dim.65), calls=%async_computation.1 | async-start | bytes 131072 | tf_op jit(solution)/shard_map/all_to_all | solution.py:133
  27.6 0.9 fusion.39
  28.5 0.8 fusion.40
  29.5 1.3 multiply_convert_fusion.3
  31.0 2.5 %multiply_convert_fusion.2 = bf16[1,256,1024]{2,1,0:T(8,128)(2,1)S(1)} fusion(bf16[1,256,1024]{2,1,0:T(8,128)(2,1)} %param.11, bf16[1,3,1024]{2,1,0:T(4,128)(2,1)S(1)} %collective-permute-done, f32[1024]{0:T(1024)S(1)} %bitcast.181, f32[1024]{0:T(1024)S(1)} %bitcast.182, f32[1024]{0:T(1024)S(1)} %bitcast.180, f32[1024]{0:T(1024)S(1)} %bitcast.179), kind=kLoop, calls=%fused_computation.35 | loop fusion | flops 6553600 | bytes 1071104 | tf_op jit(solution)/shard_map/convert_element_type | solution.py:37
  33.7 12.4 %while.14 = (s32[]{:T(128)}, f32[8,1,256,128]{2,3,1,0:T(8,128)}, f32[8,1,2,64,128]{4,3,2,1,0:T(8,128)S(1)}, bf16[8,1,256,128]{2,3,1,0:T(8,128)(2,1)S(1)}, f32[1,...) while((s32[]{:T(128)}, f32[8,1,256,128]{2,3,1,0:T(8,128)}, ...), condition=%wide.region_3.4_spmd.clone.clone, body=%wide.region_2.3_spmd.clone.clone.sunk | while | flops 26117120 | bytes 1534101 | solution.py:75
  46.7 6.4 %copy.174 = f32[1,1,16,8192]{2,1,0,3:T(1,128)} copy(f32[1,1,16,8192]{3,0,2,1:T(1,128)S(1)} %broadcast_add_fusion) | data formatting | bytes 1048576 | tf_op jit(solution)/shard_map/add | solution.py:123
  53.6 38.4 %reduce.8 = f32[8192,16]{1,0:T(8,128)} reduce(f32[8192,1,1,16]{3,2,1,0:T(1,128)} %bitcast.147, f32[]{:T(128)} %broadcast.168), dimensions={1,2}, to_apply=%bitcast.112.reduce_sub_computation | reduce | bytes 1048580
  92.0 4.2 %reshape.381 = f32[128,1,1024]{2,1,0:T(1,128)} reshape(f32[8192,16]{1,0:T(8,128)} %reduce.8) | data formatting | bytes 1048576
  96.2 13.7 %all-to-all-start = ((f32[128,1,1024]{2,1,0:T(1,128)}), f32[128,1,1024]{2,1,0:T(1,128)S(1)}, u32[]{:S(2)}, u32[]{:S(2)}) async-start(f32[128,1,1024]{2,1,0:T(1,128)} %reshape.381), calls=%async_computation | async-start | bytes 1048576 | tf_op jit(solution)/shard_map/all_to_all | solution.py:132
  111.1 19.1 %all-to-all-done = f32[128,1,1024]{2,1,0:T(1,128)S(1)} async-done(((f32[128,1,1024]{2,1,0:T(1,128)}), f32[128,1,1024]{2,1,0:T(1,128)S(1)}, u32[]{:S(2)}, u32[]{:S(2)}) %all-to-all-start) | async-done | bytes 524320 | tf_op jit(solution)/shard_map/all_to_all | solution.py:132
  130.2 1.9 reduce.9
  132.1 9.2 %reshape.382 = f32[8192,1,1,16]{3,2,1,0:T(1,128)} reshape(f32[128,1024]{1,0:T(8,128)S(1)} %reduce.9) | data formatting | bytes 1048576
  141.3 3.1 %copy.194 = f32[1,1,16,128,64]{4,3,2,1,0:T(8,128)S(1)} copy(f32[1,1,16,128,64]{2,4,3,1,0:T(8,128)} %bitcast.146) | data formatting | bytes 1048576 | tf_op jit(solution)/shard_map/all_to_all | solution.py:132
  151.5 1.0 reshape.383
  152.5 6.5 %all-to-all-start.2 = ((bf16[128,2,512]{2,1,0:T(2,128)(2,1)}), bf16[128,2,512]{2,1,0:T(2,128)(2,1)S(1)}, u32[]{:S(2)}, u32[]{:S(2)}) async-start(bf16[128,2,512]{2,1,0:T(2,128)(2,1)} %reshape.383), calls=%async_computation.2 | async-start | bytes 524288 | tf_op jit(solution)/shard_map/all_to_all | solution.py:136
  159.3 14.4 %all-to-all-done.2 = bf16[128,2,512]{2,1,0:T(2,128)(2,1)S(1)} async-done(((bf16[128,2,512]{2,1,0:T(2,128)(2,1)}), bf16[128,2,512]{2,1,0:T(2,128)(2,1)S(1)}, u32[]{:S(2)}, u32[]{:S(2)}) %all-to-all-start.2) | async-done | bytes 262176 | tf_op jit(solution)/shard_map/all_to_all | solution.py:136
  175.1 1.5 multiply_reduce_fusion
  176.6 9.4 %all_to_all.50 = f32[4,1,256]{2,1,0:T(1,128)S(1)} all-to-all(f32[4,1,256]{2,1,0:T(1,128)S(1)} %broadcast_in_dim.66), channel_id=1, replica_groups=mesh['seq'=128,'head'=4] {'head'}, dimensions={0} | all-to-all | bytes 8192 | tf_op jit(solution)/shard_map/all_to_all | solution.py:19
  186.0 0.9 multiply_convert_fusion.1
  (218 shorter events, 26.4 us)
Async XLA Ops:
  0.7 30.3 %collective-permute-start = (bf16[1,3,1024]{2,1,0:T(4,128)(2,1)S(1)}, bf16[1,3,1024]{2,1,0:T(4,128)(2,1)S(1)}, u32[]{:S(2)}, u32[]{:S(2)}) collective-permute-start(bf16[1,3,1024]{2,1,0:T(4,128)(2,1)S(1)} %slice.231), channel_id=1, source_target_pairs={{0,4},{4,8},{8,12},{12,16},{16,20},{20,24},{24,28},{28,32},{32,36}... | collective-permute-start | bytes 18440 | tf_op jit(solution)/shard_map/ppermute | solution.py:14
  3.3 26.1 %collective-permute-start.1 = (bf16[1,3,256]{2,1,0:T(4,128)(2,1)S(1)}, bf16[1,3,256]{2,1,0:T(4,128)(2,1)S(1)}, u32[]{:S(2)}, u32[]{:S(2)}) collective-permute-start(bf16[1,3,256]{2,1,0:T(4,128)(2,1)S(1)} %slice.239), channel_id=1, source_target_pairs={{0,4},{4,8},{8,12},{12,16},{16,20},{20,24},{24,28},{28,32},{32,36}... | collective-permute-start | bytes 4616 | tf_op jit(solution)/shard_map/ppermute | solution.py:14
  11.2 85.0 %all-to-all-start.1 = ((f32[1,1,16,128]{2,1,0,3:T(1,128)}), f32[1,1,16,128]{2,1,0,3:T(1,128)S(1)}, u32[]{:S(2)}, u32[]{:S(2)}) async-start(f32[1,1,16,128]{2,1,0,3:T(1,128)} %broadcast_in_dim.65), calls=%async_computation.1 | async-start | bytes 131072 | tf_op jit(solution)/shard_map/all_to_all | solution.py:133
  96.2 34.0 %all-to-all-start = ((f32[128,1,1024]{2,1,0:T(1,128)}), f32[128,1,1024]{2,1,0:T(1,128)S(1)}, u32[]{:S(2)}, u32[]{:S(2)}) async-start(f32[128,1,1024]{2,1,0:T(1,128)} %reshape.381), calls=%async_computation | async-start | bytes 1048576 | tf_op jit(solution)/shard_map/all_to_all | solution.py:132
  150.9 8.1 %copy-start = (f32[8,1,256,128]{2,3,1,0:T(8,128)S(1)}, f32[8,1,256,128]{2,3,1,0:T(8,128)}, u32[]{:S(2)}) copy-start(f32[8,1,256,128]{2,3,1,0:T(8,128)} %get-tuple-element.56) | copy-start | bytes 3145732
  152.5 21.2 %all-to-all-start.2 = ((bf16[128,2,512]{2,1,0:T(2,128)(2,1)}), bf16[128,2,512]{2,1,0:T(2,128)(2,1)S(1)}, u32[]{:S(2)}, u32[]{:S(2)}) async-start(bf16[128,2,512]{2,1,0:T(2,128)(2,1)} %reshape.383), calls=%async_computation.2 | async-start | bytes 524288 | tf_op jit(solution)/shard_map/all_to_all | solution.py:136
  174.2 11.8 %copy-start.1 = (f32[1024]{0:T(1024)S(1)}, f32[1024]{0:T(1024)}, u32[]{:S(2)}) copy-start(f32[1024]{0:T(1024)} %param.19) | copy-start | bytes 12292
where the time goes:
time: 188 us; the launch traced here: 187 us
  other arithmetic  52.2 us (28%)
  local copies, waits for them, and re-layouts  43.5 us (23%)
  starting transfers between devices  43 us (23%)
  waiting for transfers between devices  33.4 us (18%)
  blocking collectives  9.39 us (5%)
  matrix products  4.3 us (2%)
    unnamed x2, other arithmetic  39.2 us
    all_to_all x1, waiting for transfers between devices, shards(): lax.all_to_all(flat_state, 'seq', split_axis=3, concat_axis=0, tiled=True)  19.1 us
    all_to_all x1, starting transfers between devices, shards(): lax.all_to_all(spread_decay, 'seq', split_axis=3, concat_axis=0, tiled=True)  16.5 us
    unnamed x12, local copies, waits for them, and re-layouts  15.9 us
    all_to_all x1, waiting for transfers between devices, shards(): lax.all_to_all(exclusive, 'seq', split_axis=0, concat_axis=3, tiled=True)  14.4 us
    all_to_all x1, starting transfers between devices, shards(): lax.all_to_all(flat_state, 'seq', split_axis=3, concat_axis=0, tiled=True)  13.7 us
    all_to_all x1, blocking collectives, sent_to_all(): lax.all_to_all(jnp.broadcast_to(array[None], (count, *array.shape)), axis...  9.39 us
    all_to_all x1, starting transfers between devices, shards(): lax.all_to_all(exclusive, 'seq', split_axis=0, concat_axis=3, tiled=True)  6.48 us
  transfers between devices with their start and end apart: 5, of which 2 were waited for; matrix products, arithmetic and copies ran while one was open for 39% of the time, Pallas kernels for 0%

commit v1 on v0

v1 whole, which is shorter than its diff:
```python
import jax
import jax.numpy as jnp
from jax import lax
from jax.experimental import pallas as pl
from jax.experimental.pallas import tpu as pltpu
from jax.sharding import Mesh, PartitionSpec as P

HEADS = 64
HEAD_DIM = 64
TOKENS_LOCAL = 256
CHANNELS = 1024
HALF = 512
STATE = 128
HEADS_LOCAL = 16
CHIPS = 64
LOG2E = 1.4426950408889634
F32 = jnp.float32
BF16 = jnp.bfloat16


def silu(value):
    half = 0.5 * value
    return half + half * jnp.tanh(half)


def parts_of(value):
    high = value.astype(BF16)
    rest = value - high.astype(F32)
    middle = rest.astype(BF16)
    low = (rest - middle.astype(F32)).astype(BF16)
    return high, middle, low


def dot(left, right, dims=((1,), (0,))):
    return lax.dot_general(left, right, (dims, ((), ())), preferred_element_type=F32)


def conv_silu(values, taps):
    values = values.astype(F32)
    running = values * taps[0:1]
    for k in range(1, 4):
        running = pltpu.roll(running, 1, 0) + values * taps[k : k + 1]
    return silu(running).astype(BF16)


def conv_first(ext_ref, taps, width):
    at = slice(0, width)
    running = ext_ref[5:13, at] * taps[0:1]
    for k in range(1, 4):
        running = running + ext_ref[5 + k : 13 + k, at] * taps[k : k + 1]
    return silu(running).astype(BF16)


def copy_all(pairs, sems):
    copies = [
        pltpu.make_async_copy(source, target, sems.at[place])
        for place, (source, target) in enumerate(pairs)
    ]
    for copy in copies:
        copy.start()
    return copies


def column_of(row):
    first = lax.broadcasted_iota(jnp.int32, (HEADS_LOCAL, HEADS_LOCAL), 0)
    second = lax.broadcasted_iota(jnp.int32, (HEADS_LOCAL, HEADS_LOCAL), 1)
    return jnp.sum(jnp.where(first == second, row, 0.0), axis=1, keepdims=True)


def prepare(
    x_ref, proj_ref, step_ref, bias_ref, rate_ref, tapx_ref, tapp_ref,
    step_out_ref, log_rows_ref, log_columns_ref, factor_ref, now_ref,
    near_x, near_proj, to_end_ref, end_ref, near_tapx, near_tapp,
    near_step, near_bias, near_rate, sems, tail_ref=None,
):
    pairs = [(step_ref, near_step), (bias_ref, near_bias), (rate_ref, near_rate)]
    if tail_ref is not None:
        rows = pl.ds(TOKENS_LOCAL - 8, 8)
        pairs += [
            (x_ref.at[rows], tail_ref.at[:, pl.ds(0, CHANNELS)]),
            (proj_ref.at[rows], tail_ref.at[:, pl.ds(CHANNELS, 2 * STATE)]),
        ]
    pairs += [
        (proj_ref, near_proj),
        (x_ref, near_x),
        (tapx_ref, near_tapx),
        (tapp_ref, near_tapp),
    ]
    copies = copy_all(pairs, sems)
    row = lax.broadcasted_iota(jnp.int32, (TOKENS_LOCAL, TOKENS_LOCAL), 0)
    col = lax.broadcasted_iota(jnp.int32, (TOKENS_LOCAL, TOKENS_LOCAL), 1)
    upper = (row <= col).astype(BF16)
    head = lax.broadcasted_iota(jnp.int32, (3 * HEADS_LOCAL, CHANNELS), 0)
    channel = lax.broadcasted_iota(jnp.int32, (3 * HEADS_LOCAL, CHANNELS), 1)
    spread = (channel // HEAD_DIM == head % HEADS_LOCAL).astype(BF16)

    def stacked(value):
        return jnp.concatenate(parts_of(value), axis=0)

    def to_channels(value):
        return dot(stacked(value), spread, ((0,), (0,)))

    for copy in copies[:3]:
        copy.wait()
    raw = near_step[...] + column_of(near_bias[...])
    step = jnp.maximum(raw, 0.0) + jnp.log1p(jnp.exp(-jnp.abs(raw)))
    sums = dot(stacked(step * -column_of(near_rate[...])), upper)
    log_decay = sums[:HEADS_LOCAL] + sums[HEADS_LOCAL : 2 * HEADS_LOCAL] + sums[2 * HEADS_LOCAL :]
    step_out_ref[...] = step
    log2 = log_decay * LOG2E
    log_rows_ref[...] = log2
    pad = jnp.zeros((128 - HEADS_LOCAL, TOKENS_LOCAL), F32)
    log_columns_ref[...] = jnp.transpose(jnp.concatenate([log2, pad], axis=0))
    last = log_decay[:, TOKENS_LOCAL - 1 :]
    to_end_ref[...] = to_channels(jnp.exp(last - log_decay) * step)
    factor_ref[...] = to_channels(jnp.broadcast_to(jnp.exp(last), (HEADS_LOCAL, 8)))
    now_ref[...] = to_channels(jnp.exp(log_decay))
    token = lax.broadcasted_iota(jnp.int32, (8, 1), 0)
    end_ref[...] = jnp.where(token < 3, to_end_ref[:8], 0.0)
    to_end_ref[:8] = jnp.where(token < 3, 0.0, to_end_ref[:8])
    for copy in copies[3:]:
        copy.wait()


def early_kernel(*refs):
    inputs, tail_ref, rest = refs[:7], refs[7], refs[8:]

    @pl.when(lax.axis_index("core") == 1)
    def _():
        prepare(*inputs, *rest, tail_ref=tail_ref)


def state_kernel(*refs):
    inputs, rest = refs[:7], refs[18:]
    outputs, (xm_ref, pm_ref, sums_ref, send_ref), scratch = rest[:11], rest[11:15], rest[15:]
    factor_ref = outputs[3]
    near_x, near_proj, to_end_ref, end_ref, tapx_ref, tapp_ref = outputs[5:11]
    core = lax.axis_index("core")

    @pl.when(core == 0)
    def _():
        prepare(*inputs, *outputs, *scratch)

    is_first = first_core()
    pm = conv_silu(near_proj[...], tapp_ref[...])
    pm_ref[...] = pm
    turned = jnp.transpose(pm[:, :STATE].astype(F32)).astype(BF16)
    width = 256
    for tile in range(CHANNELS // width):
        at = slice(tile * width, (tile + 1) * width)
        xm = conv_silu(near_x[:, at], tapx_ref[:, at])
        xm_ref[:, at] = xm
        weighted = (xm.astype(F32) * to_end_ref[:, at]).astype(BF16)
        half, inside = divmod(tile * width, HALF)
        sums_ref[half, :STATE, inside : inside + width] = dot(turned, weighted)
    head_x = near_x[:8].astype(F32)
    head_proj = near_proj[:8].astype(F32)
    tail_x = near_x[-8:].astype(F32)
    tail_proj = near_proj[-8:].astype(F32)
    for half in range(2):
        at = slice(half * HALF, (half + 1) * HALF)
        sums_ref[half, STATE : STATE + 8] = factor_ref[:, at]
        sums_ref[half, STATE + 8 : STATE + 16] = jnp.where(
            is_first, tail_x[:, :HALF], head_x[:, at]
        )
        sums_ref[half, STATE + 16 : STATE + 24] = jnp.where(
            is_first, tail_x[:, HALF:], end_ref[:, at]
        )
        sums_ref[half, STATE + 24 :, : 2 * STATE] = jnp.where(is_first, tail_proj, head_proj)
        sums_ref[half, STATE + 24 :, 2 * STATE :] = jnp.zeros((8, HALF - 2 * STATE), F32)
    send_ref[...] = sums_ref[1 - core]


def first_of(halo_x, halo_proj, head_x, head_proj, tapx, tapp, ext_ref, extp_ref):
    width = halo_x.shape[1]
    ext_ref[:8] = halo_x
    ext_ref[8:] = head_x
    extp_ref[:8] = halo_proj
    extp_ref[8:] = head_proj
    pm = conv_first(extp_ref, tapp, 2 * STATE)
    return conv_first(ext_ref, tapx, width), pm


def first_core():
    return jnp.full((1, 1), lax.axis_index("core"), jnp.int32) == 0


def first_kernel(
    halo_ref, x_ref, proj_ref, end_ref, tapx_ref, tapp_ref, own_ref, send_ref, ext_ref, extp_ref
):
    halo = halo_ref[...].astype(F32)
    xm, pm = first_of(
        halo[:, :CHANNELS], halo[:, CHANNELS:], x_ref[:8].astype(F32), proj_ref[:8].astype(F32),
        tapx_ref[...], tapp_ref[...], ext_ref, extp_ref,
    )
    weighted = (xm.astype(F32) * end_ref[...]).astype(BF16)
    own_ref[:, :HALF] = weighted[:, :HALF]
    own_ref[:, HALF:] = pm[:, :STATE]
    send_ref[:, :HALF] = weighted[:, HALF:]
    send_ref[:, HALF:] = pm[:, :STATE]


def join_kernel(
    sums_ref, recv_ref, x_ref, proj_ref, tapx_ref, tapp_ref, own_rows_ref, recv_rows_ref,
    message_ref, first_ref, ext_ref, extp_ref,
):
    core = lax.axis_index("core")
    is_first = first_core()
    own = sums_ref[core]
    other = recv_ref[...]
    tail_x = x_ref[-8:].astype(F32)
    tail_proj = proj_ref[-8:].astype(F32)
    taps = tapx_ref[...]
    xm, pm = first_of(
        jnp.where(is_first, tail_x[:, :HALF], other[STATE + 16 : STATE + 24]),
        jnp.where(is_first, tail_proj, other[STATE + 24 :, : 2 * STATE]),
        jnp.where(is_first, other[STATE + 8 : STATE + 16], own[STATE + 8 : STATE + 16]),
        jnp.where(is_first, other[STATE + 24 :, : 2 * STATE], own[STATE + 24 :, : 2 * STATE]),
        jnp.where(is_first, taps[:, :HALF], taps[:, HALF:]),
        tapp_ref[...],
        ext_ref,
        extp_ref,
    )
    end = jnp.where(is_first, other[STATE + 16 : STATE + 24], own[STATE + 16 : STATE + 24])
    added = dot(pm[:, :STATE], (xm.astype(F32) * end).astype(BF16), ((0,), (0,)))
    rows = jnp.where(
        is_first, own_rows_ref[...].astype(F32), recv_rows_ref[...].astype(F32)
    ).astype(BF16)
    added_first = dot(rows[:, HALF:], rows[:, :HALF], ((0,), (0,)))
    first = jnp.where(is_first, own[: STATE + 8], other[: STATE + 8])
    second = jnp.where(is_first, other[: STATE + 8], own[: STATE + 8])
    first_state = first[:STATE] + added_first
    first_ref[:STATE] = first_state
    first_ref[STATE:] = first[STATE:]
    factor = second[STATE:] * first[STATE:]
    total = second[STATE : STATE + 1] * first_state + (second[:STATE] + added)
    high = factor.astype(BF16)
    low = (factor - high.astype(F32)).astype(BF16)
    row = lax.broadcasted_iota(jnp.int32, (8, HALF), 0)
    tags = jnp.where(row == 0, high.astype(F32), low.astype(F32)).astype(BF16)
    total = total.astype(BF16)
    for group in range(STATE // 8):
        for lane in range(HALF // 128):
            at = slice(lane * 128, (lane + 1) * 128)
            slot = group * (HALF // 128) + lane
            for piece in range(4):
                start = group * 8 + piece * 2
                message_ref[slot, piece] = total[start : start + 2, at]
            message_ref[slot, 4] = tags[0:2, at]


def scan_kernel(message_ref, out_ref):
    carried = [jnp.zeros((2, 128), F32) for _ in range(4)]
    for chip in range(CHIPS):
        tags = message_ref[chip, 4].astype(F32)
        factor = tags[0:1] + tags[1:2]
        for piece in range(4):
            high = carried[piece].astype(BF16)
            out_ref[chip, piece] = high
            out_ref[chip, piece + 4] = (carried[piece] - high.astype(F32)).astype(BF16)
            carried[piece] = factor * carried[piece] + message_ref[chip, piece].astype(F32)


def enter_kernel(came_ref, first_ref, keep_ref, send_ref):
    core = lax.axis_index("core")
    is_first = jnp.full((1, 1), core, jnp.int32) == 0
    for group in range(STATE // 8):
        for lane in range(HALF // 128):
            at = slice(lane * 128, (lane + 1) * 128)
            rows = slice(group * 8, group * 8 + 8)
            slot = group * (HALF // 128) + lane
            even = jnp.concatenate(
                [
                    came_ref[slot, piece].astype(F32) + came_ref[slot, piece + 4].astype(F32)
                    for piece in range(4)
                ],
                axis=0,
            )
            odd = first_ref[STATE : STATE + 1, at] * even + first_ref[rows, at]
            keep_ref[rows, at] = jnp.where(is_first, even, odd).astype(BF16)
            send_ref[rows, at] = jnp.where(is_first, odd, even).astype(BF16)


def within_kernel(
    early_ref, pm_ref, step_rows, log_rows, log_columns, now_ref, gate_ref, halo_ref, recv_ref,
    x_ref, proj_ref, tapx_ref, tapp_ref, within_ref, read_ref, outer_ref, xm_ref, write_ref,
    ext_ref, extp_ref,
):
    is_first = first_core()
    halo = halo_ref[...].astype(F32)
    came = jnp.concatenate(
        [
            recv_ref[STATE + 8 : STATE + 16],
            recv_ref[STATE + 16 : STATE + 24],
            recv_ref[STATE + 24 :, : 2 * STATE],
        ],
        axis=1,
    )
    halo = jnp.where(is_first, halo, came)
    xm, pm = first_of(
        halo[:, :CHANNELS], halo[:, CHANNELS:], x_ref[:8].astype(F32), proj_ref[:8].astype(F32),
        tapx_ref[...], tapp_ref[...], ext_ref, extp_ref,
    )
    token = lax.broadcasted_iota(jnp.int32, (8, 1), 0)

    def with_first(new, old):
        return jnp.where(token < 3, new.astype(F32), old.astype(F32)).astype(BF16)

    xm_ref[:8] = with_first(xm, early_ref[:8])
    xm_ref[8:] = early_ref[8:]
    pm = with_first(pm, pm_ref[:8])
    write_ref[:8] = pm[:, :STATE]
    write_ref[8:] = pm_ref[8:, :STATE]
    read_ref[:8] = pm[:, STATE:]
    read_ref[8:] = pm_ref[8:, STATE:]
    scores = dot(read_ref[...], write_ref[...], ((1,), (1,)))
    row = lax.broadcasted_iota(jnp.int32, (128, 128), 0)
    col = lax.broadcasted_iota(jnp.int32, (128, 128), 1)
    causal = col <= row
    left = lax.broadcasted_iota(jnp.int32, (128, 128), 1) < HEAD_DIM
    for pair in range(HEADS_LOCAL // 2):
        at = slice(pair * 128, (pair + 1) * 128)
        outs = []
        for head in (2 * pair, 2 * pair + 1):
            tops = []
            for t in range(2):
                parts = []
                trow = slice(t * 128, (t + 1) * 128)
                log_t = log_columns[trow, head : head + 1]
                for s in range(t + 1):
                    scol = slice(s * 128, (s + 1) * 128)
                    gap = log_t - log_rows[head : head + 1, scol]
                    if s == t:
                        gap = jnp.where(causal, gap, 0.0)
                    mix = scores[trow, scol] * jnp.exp2(gap) * step_rows[head : head + 1, scol]
                    if s == t:
                        mix = jnp.where(causal, mix, 0.0)
                    parts.append(mix.astype(BF16))
                mixing = parts[0] if t == 0 else jnp.concatenate(parts, axis=1)
                tops.append(dot(mixing, xm_ref[: (t + 1) * 128, at]))
            outs.append(tops)
        for t in range(2):
            trow = slice(t * 128, (t + 1) * 128)
            gates = silu(gate_ref[trow, at].astype(F32))
            outer_ref[trow, at] = now_ref[trow, at] * gates
            within_ref[trow, at] = jnp.where(left, outs[0][t], outs[1][t]) * gates


def gate_kernel(keep_ref, recv_ref, read_ref, within_ref, outer_ref, gated_ref, square_ref):
    core = lax.axis_index("core")
    is_first = jnp.full((1, 1), core, jnp.int32) == 0
    partial = jnp.zeros((TOKENS_LOCAL, 128), F32)
    for half in range(2):
        at = slice(half * HALF, (half + 1) * HALF)
        if half == 0:
            state = jnp.where(is_first, keep_ref[...], recv_ref[...])
        else:
            state = jnp.where(is_first, recv_ref[...], keep_ref[...])
        gated = within_ref[:, at] + outer_ref[:, at] * dot(read_ref[...], state)
        gated_ref[:, at] = gated
        square = gated * gated
        for lane in range(HALF // 128):
            partial = partial + square[:, lane * 128 : (lane + 1) * 128]
    total = jnp.sum(jnp.transpose(partial), axis=0, keepdims=True)
    row = lax.broadcasted_iota(jnp.int32, (8, 128), 0)
    block = jnp.where(row == 0, total[:, :128], jnp.where(row == 1, total[:, 128:], 0.0))
    for peer in range(4):
        square_ref[peer] = block


def norm_kernel(gated_ref, square_ref, gain_ref, out_ref, near_out_ref, sems):
    total = jnp.sum(square_ref[...], axis=0)
    scale = lax.rsqrt(total / (HEADS * HEAD_DIM) + 1.0)
    wide = jnp.concatenate(
        [jnp.broadcast_to(scale[0:1], (128, 128)), jnp.broadcast_to(scale[1:2], (128, 128))], axis=1
    )
    column = jnp.transpose(wide)
    chunks = 4
    size = TOKENS_LOCAL // chunks
    copies = []
    for chunk in range(chunks):
        rows = slice(chunk * size, (chunk + 1) * size)
        for lane in range(CHANNELS // 128):
            at = slice(lane * 128, (lane + 1) * 128)
            near_out_ref[rows, at] = (
                gated_ref[rows, at] * column[rows] * gain_ref[:, at]
            ).astype(BF16)
        here = pl.ds(chunk * size, size)
        copies.append(
            pltpu.make_async_copy(near_out_ref.at[here], out_ref.at[here], sems.at[chunk])
        )
        copies[-1].start()
    for copy in copies:
        copy.wait()


def shape(dims, dtype):
    return pltpu.VMEM(dims, dtype)


def call(kernel, outs, scratch=(), flops=0, **specs):
    cost = pl.CostEstimate(flops=flops, transcendentals=0, bytes_accessed=0) if flops else None
    return pl.pallas_call(
        kernel,
        out_shape=outs,
        scratch_shapes=scratch,
        cost_estimate=cost,
        compiler_params=pltpu.CompilerParams(vmem_limit_bytes=24 * 1024 * 1024),
        **specs,
    )


def near(value):
    return pltpu.with_memory_space_constraint(value, pltpu.VMEM)


def far(value):
    return pltpu.with_memory_space_constraint(value, pltpu.HBM)


ANY = pl.BlockSpec(memory_space=pl.ANY)
NEAR = pl.BlockSpec(memory_space=pltpu.VMEM)


def shards(
    seq_inputs, gate_inputs, projections, step_raw, step_bias, decay_rate, conv_feature, conv_proj,
    norm_gain,
):
    x = far(seq_inputs[0])
    proj = far(projections[0])
    step_rows = jnp.transpose(step_raw[0])
    chips = ("y", "z")
    rows = STATE + 32
    whole = (TOKENS_LOCAL, CHANNELS)
    prepared = (
        shape((HEADS_LOCAL, TOKENS_LOCAL), F32),
        shape((HEADS_LOCAL, TOKENS_LOCAL), F32),
        shape((TOKENS_LOCAL, 128), F32),
        shape((8, CHANNELS), F32),
        shape(whole, F32),
        shape(whole, BF16),
        shape((TOKENS_LOCAL, 2 * STATE), BF16),
        shape(whole, F32),
        shape((8, CHANNELS), F32),
        shape((4, CHANNELS), F32),
        shape((4, 2 * STATE), F32),
    )
    sources = (
        x, proj, far(step_rows), far(step_bias[None]), far(decay_rate[None]),
        far(conv_feature), far(conv_proj),
    )
    loads = [
        pltpu.VMEM((HEADS_LOCAL, TOKENS_LOCAL), F32),
        pltpu.VMEM((1, HEADS_LOCAL), F32),
        pltpu.VMEM((1, HEADS_LOCAL), F32),
        pltpu.SemaphoreType.DMA((9,)),
    ]
    tail, *early = call(
        early_kernel,
        (shape((8, CHANNELS + 2 * STATE), BF16),) + prepared,
        loads,
        in_specs=[ANY] * 7,
    )(*sources)
    halo = lax.ppermute(tail, ("y", "z", "core"), [(i, i + 1) for i in range(1, 2 * CHIPS - 1, 2)])
    (
        step, log_rows, log_columns, _, now, near_x, near_proj, _, end, tapx, tapp,
        xm, pm, sums, send,
    ) = call(
        state_kernel,
        prepared
        + (
            shape(whole, BF16),
            shape((TOKENS_LOCAL, 2 * STATE), BF16),
            shape((2, rows, HALF), F32),
            shape((rows, HALF), F32),
        ),
        loads,
        10**9,
        in_specs=[ANY] * 7 + [NEAR] * 11,
        input_output_aliases={7 + i: i for i in range(11)},
    )(*sources, *(near(value) for value in early))
    swap = [(0, 1), (1, 0)]
    other = lax.ppermute(send, "core", swap)
    small = [pltpu.VMEM((16, CHANNELS), F32), pltpu.VMEM((16, 2 * STATE), F32)]
    ranks = shape((8, HALF + STATE), BF16)
    own_rows, rows_send = call(first_kernel, (ranks, ranks), small)(
        near(halo), near(near_x), near(near_proj), near(end), near(tapx), near(tapp)
    )
    came_rows = lax.ppermute(rows_send, "core", [(0, 1)])
    message, first = call(
        join_kernel,
        (shape((CHIPS, 5, 2, 128), BF16), shape((STATE + 8, HALF), F32)),
        [pltpu.VMEM((16, HALF), F32), pltpu.VMEM((16, 2 * STATE), F32)],
    )(
        near(sums), near(other), near(near_x), near(near_proj), near(tapx), near(tapp),
        near(own_rows), near(came_rows),
    )
    gathered = lax.all_to_all(message, chips, 0, 0, tiled=True)
    entering = call(scan_kernel, shape((CHIPS, 8, 2, 128), BF16))(near(gathered))
    returned = lax.all_to_all(entering, chips, 0, 0, tiled=True)
    keep, give = call(
        enter_kernel, (shape((STATE, HALF), BF16), shape((STATE, HALF), BF16))
    )(near(returned), near(first))
    got = lax.ppermute(give, "core", swap)
    within, read, outer = call(
        within_kernel,
        (shape(whole, F32), shape((TOKENS_LOCAL, STATE), BF16), shape(whole, F32)),
        [pltpu.VMEM(whole, BF16), pltpu.VMEM((TOKENS_LOCAL, STATE), BF16)] + small,
        10**10,
    )(
        near(xm), near(pm), near(step), near(log_rows), near(log_columns), near(now),
        gate_inputs[0], near(halo), near(other), near(near_x), near(near_proj), near(tapx),
        near(tapp),
    )
    gated, square = call(
        gate_kernel, (shape((TOKENS_LOCAL, CHANNELS), F32), shape((4, 8, 128), F32))
    )(near(keep), near(got), near(read), near(within), near(outer))
    squares = lax.all_to_all(square, "head", 0, 0, tiled=True)
    out = call(
        norm_kernel,
        pltpu.HBM((TOKENS_LOCAL, CHANNELS), BF16),
        [pltpu.VMEM((TOKENS_LOCAL, CHANNELS), BF16), pltpu.SemaphoreType.DMA((4,))],
        out_specs=ANY,
    )(near(gated), near(squares), norm_gain[None])
    return out[None]


def solution(mesh):
    grid = Mesh(mesh.devices.reshape(8, 8, 2, 4), ("y", "z", "core", "head"))
    seq = ("y", "z", "core")
    return jax.shard_map(
        shards,
        mesh=grid,
        in_specs=(
            P(None, seq, "head"),
            P(None, seq, "head"),
            P(None, seq, None),
            P(None, seq, "head"),
            P("head"),
            P("head"),
            P(None, "head"),
            P(),
            P("head"),
        ),
        out_specs=P(None, seq, "head"),
        check_vma=False,
    )
```

time: 188 us -> 77.1 us (0.41)
  the two profiles are of different devices: /device:TPU:8 before, /device:TPU:1 now
where the time goes in v1:
time: 77.1 us; the launch traced here: 76.8 us
  blocking collectives  50.7 us (66%)
  starting transfers between devices  16.7 us (22%)
  Pallas kernels  6.55 us (8%)
  waiting for transfers between devices  2.66 us (3%)
    all_to_all x1, blocking collectives, shards(): gathered = lax.all_to_all(message, chips, 0, 0, tiled=True)  25.5 us
    all_to_all x1, blocking collectives, shards(): returned = lax.all_to_all(entering, chips, 0, 0, tiled=True)  17.2 us
    ppermute x1, starting transfers between devices, shards(): other = lax.ppermute(send, 'core', swap)  8.74 us
    all_to_all x1, blocking collectives, shards(): squares = lax.all_to_all(square, 'head', 0, 0, tiled=True)  8.03 us
    ppermute x1, starting transfers between devices, shards(): got = lax.ppermute(give, 'core', swap)  5.38 us
    ppermute x1, waiting for transfers between devices, shards(): came_rows = lax.ppermute(rows_send, 'core', [(0, 1)])  1.77 us
    pallas_call x1, Pallas kernels, shards(): call(early_kernel, (shape((8, CHANNELS + 2 * STATE), BF16),) + prepared,...  1.61 us
  transfers between devices with their start and end apart: 4, of which 2 were waited for; matrix products, arithmetic and copies ran while one was open for 0% of the time, Pallas kernels for 2%

profile of v1, /device:TPU:1, one launch (start us, length us, event | category | flops | bytes accessed | tf_op | source)
XLA Modules:
  0.0 76.8 jit_solution(8032134090664975380)
XLA Ops:
  0.0 1.6 %shard_map.91 = (bf16[8,1280]{1,0:T(8,128)(2,1)S(1)}, f32[16,256]{1,0:T(8,128)S(1)}, f32[16,256]{1,0:T(8,128)S(1)}, f32[256,128]{1,0:T(8,128)S(1)}, f32[8,1024]{...) custom-call(bf16[256,1024]{1,0:T(8,128)(2,1)} %bitcast.12, ...), custom_call_target="tpu_custom_call" | custom-call | tf_op jit(solution)/shard_map/pallas_call | solution.py:458
  1.6 1.3 %shard_map.92 = (f32[16,256]{1,0:T(8,128)S(1)}, f32[16,256]{1,0:T(8,128)S(1)}, f32[256,128]{1,0:T(8,128)S(1)}, f32[8,1024]{1,0:T(8,128)S(1)}, f32[256,1024]{1,0:...) custom-call(bf16[256,1024]{1,0:T(8,128)(2,1)} %bitcast.13, ...), custom_call_target="tpu_custom_call", output_to_operand_aliasing={{0}: (7, {}), {1}: (8, {}), {2}: (9, {}), {3}: (10, {}), {4... | custom-call | flops 1000000000 | tf_op jit(solution)/shard_map/pallas_call | solution.py:468
  3.0 8.7 %collective-permute-start = (f32[160,512]{1,0:T(8,128)S(1)}, f32[160,512]{1,0:T(8,128)S(1)}, u32[]{:S(2)}, u32[]{:S(2)}) collective-permute-start(f32[160,512]{1,0:T(8,128)S(1)} %get-tuple-element.53), channel_id=1, source_target_pairs={{0,4},{4,0},{1,5},{5,1},{2,6},{6,2},{3,7},{7,3},{8,12},{12,8},{9,1... | collective-permute-start | bytes 983048 | tf_op jit(solution)/shard_map/ppermute | solution.py:483
  11.7 1.3 %collective-permute-start.1 = (bf16[8,1280]{1,0:T(8,128)(2,1)S(1)}, bf16[8,1280]{1,0:T(8,128)(2,1)S(1)}, u32[]{:S(2)}, u32[]{:S(2)}) collective-permute-start(bf16[8,1280]{1,0:T(8,128)(2,1)S(1)} %get-tuple-element.58), channel_id=1, source_target_pairs={{4,8},{12,16},{20,24},{28,32},{36,40},{44,48},{52,56},{60,64},{68,... | collective-permute-start | bytes 61448 | tf_op jit(solution)/shard_map/ppermute | solution.py:464
  13.0 0.9 %collective-permute-done.1.halo_ref = bf16[8,1280]{1,0:T(8,128)(2,1)S(1)} collective-permute-done((bf16[8,1280]{1,0:T(8,128)(2,1)S(1)}, bf16[8,1280]{1,0:T(8,128)(2,1)S(1)}, u32[]{:S(2)}, u32[]{:S(2)}) %collective-permute-start.1) | collective-permute-done | bytes 20512 | tf_op jit(solution)/shard_map/ppermute | solution.py:464
  13.9 0.1 shard_map.93
  14.0 1.3 %collective-permute-start.2 = (bf16[8,640]{1,0:T(8,128)(2,1)S(1)}, bf16[8,640]{1,0:T(8,128)(2,1)S(1)}, u32[]{:S(2)}, u32[]{:S(2)}) collective-permute-start(bf16[8,640]{1,0:T(8,128)(2,1)S(1)} %get-tuple-element.61), channel_id=1, source_target_pairs={{0,4},{1,5},{2,6},{3,7},{8,12},{9,13},{10,14},{11,15},{16,20},{17,... | collective-permute-start | bytes 30728 | tf_op jit(solution)/shard_map/ppermute | solution.py:489
  15.3 1.8 %collective-permute-done.2.recv_rows_ref = bf16[8,640]{1,0:T(8,128)(2,1)S(1)} collective-permute-done((bf16[8,640]{1,0:T(8,128)(2,1)S(1)}, bf16[8,640]{1,0:T(8,128)(2,1)S(1)}, u32[]{:S(2)}, u32[]{:S(2)}) %collective-permute-start.2) | collective-permute-done | bytes 10272 | tf_op jit(solution)/shard_map/ppermute | solution.py:489
  17.0 0.0 collective-permute-done.recv_ref
  17.0 0.4 shard_map.94
  17.4 25.5 %all_to_all.15.message_ref = bf16[64,5,2,128]{3,2,1,0:T(2,128)(2,1)S(1)} all-to-all(bf16[64,5,2,128]{3,2,1,0:T(2,128)(2,1)S(1)} %get-tuple-element.62), channel_id=1, replica_groups=mesh['y'=8,'z'=8,'core'=2,'head'=4] {'y','z'}, dimensions={0} | all-to-all | bytes 327680 | tf_op jit(solution)/shard_map/all_to_all | solution.py:498
  42.9 0.3 shard_map.95
  43.2 0.0 copy-start.1
  43.2 17.2 %all_to_all.16.came_ref = bf16[64,8,2,128]{3,2,1,0:T(2,128)(2,1)S(1)} all-to-all(bf16[64,8,2,128]{3,2,1,0:T(2,128)(2,1)S(1)} %shard_map.95), channel_id=1, replica_groups=mesh['y'=8,'z'=8,'core'=2,'head'=4] {'y','z'}, dimensions={0} | all-to-all | bytes 524288 | tf_op jit(solution)/shard_map/all_to_all | solution.py:500
  60.4 0.2 shard_map.96
  60.7 5.4 %collective-permute-start.3 = (bf16[128,512]{1,0:T(8,128)(2,1)S(1)}, bf16[128,512]{1,0:T(8,128)(2,1)S(1)}, u32[]{:S(2)}, u32[]{:S(2)}) collective-permute-start(bf16[128,512]{1,0:T(8,128)(2,1)S(1)} %get-tuple-element.65), channel_id=1, source_target_pairs={{0,4},{4,0},{1,5},{5,1},{2,6},{6,2},{3,7},{7,3},{8,12},{12,8},{9,1... | collective-permute-start | bytes 393224 | tf_op jit(solution)/shard_map/ppermute | solution.py:504
  66.1 0.0 copy-done.1
  66.1 1.3 %shard_map.97 = (f32[256,1024]{1,0:T(8,128)S(1)}, bf16[256,128]{1,0:T(8,128)(2,1)S(1)}, f32[256,1024]{1,0:T(8,128)S(1)}) custom-call(bf16[256,1024]{1,0:T(8,128)(2,1)S(1)} %get-tuple-element.66.early_ref, bf16[256,256]{1,0:T(8,128)(2,1)S(1)} %get-tuple-element.67.pm_ref, f32[16,256]{1,0:T(8,128)S(1)} %get-tuple-element.68.step_rows, ...), custom_call_target="tpu_custom_call" | custom-call | flops 10000000000 | tf_op jit(solution)/shard_map/pallas_call | solution.py:505
  67.4 0.0 collective-permute-done.3.recv_ref
  67.4 0.4 shard_map.98
  67.8 0.0 copy-start
  67.8 8.0 %all_to_all.17.square_ref = f32[4,8,128]{2,1,0:T(8,128)S(1)} all-to-all(f32[4,8,128]{2,1,0:T(8,128)S(1)} %get-tuple-element.76), channel_id=1, replica_groups=mesh['y'=8,'z'=8,'core'=2,'head'=4] {'head'}, dimensions={0} | all-to-all | bytes 32768 | tf_op jit(solution)/shard_map/all_to_all | solution.py:518
  75.8 0.0 copy-done
  75.8 1.0 %shard_map.99 = bf16[256,1024]{1,0:T(8,128)(2,1)} custom-call(f32[256,1024]{1,0:T(8,128)S(1)} %get-tuple-element.75.gated_ref, f32[4,8,128]{2,1,0:T(8,128)S(1)} %all_to_all.17.square_ref, f32[1,1024]{1,0:T(1,128)S(1)} %bitcast.10), custom_call_target="tpu_custom_call" | custom-call | tf_op jit(solution)/shard_map/pallas_call | solution.py:519
Async XLA Ops:
  3.0 14.1 %collective-permute-start = (f32[160,512]{1,0:T(8,128)S(1)}, f32[160,512]{1,0:T(8,128)S(1)}, u32[]{:S(2)}, u32[]{:S(2)}) collective-permute-start(f32[160,512]{1,0:T(8,128)S(1)} %get-tuple-element.53), channel_id=1, source_target_pairs={{0,4},{4,0},{1,5},{5,1},{2,6},{6,2},{3,7},{7,3},{8,12},{12,8},{9,1... | collective-permute-start | bytes 983048 | tf_op jit(solution)/shard_map/ppermute | solution.py:483
  11.7 2.2 %collective-permute-start.1 = (bf16[8,1280]{1,0:T(8,128)(2,1)S(1)}, bf16[8,1280]{1,0:T(8,128)(2,1)S(1)}, u32[]{:S(2)}, u32[]{:S(2)}) collective-permute-start(bf16[8,1280]{1,0:T(8,128)(2,1)S(1)} %get-tuple-element.58), channel_id=1, source_target_pairs={{4,8},{12,16},{20,24},{28,32},{36,40},{44,48},{52,56},{60,64},{68,... | collective-permute-start | bytes 61448 | tf_op jit(solution)/shard_map/ppermute | solution.py:464
  14.0 3.1 %collective-permute-start.2 = (bf16[8,640]{1,0:T(8,128)(2,1)S(1)}, bf16[8,640]{1,0:T(8,128)(2,1)S(1)}, u32[]{:S(2)}, u32[]{:S(2)}) collective-permute-start(bf16[8,640]{1,0:T(8,128)(2,1)S(1)} %get-tuple-element.61), channel_id=1, source_target_pairs={{0,4},{1,5},{2,6},{3,7},{8,12},{9,13},{10,14},{11,15},{16,20},{17,... | collective-permute-start | bytes 30728 | tf_op jit(solution)/shard_map/ppermute | solution.py:489
  43.2 22.9 %copy-start.1 = (bf16[1,256,1024]{2,1,0:T(8,128)(2,1)S(1)}, bf16[1,256,1024]{2,1,0:T(8,128)(2,1)}, u32[]{:S(2)}) copy-start(bf16[1,256,1024]{2,1,0:T(8,128)(2,1)} %param.10) | copy-start | bytes 1572868
  60.7 6.7 %collective-permute-start.3 = (bf16[128,512]{1,0:T(8,128)(2,1)S(1)}, bf16[128,512]{1,0:T(8,128)(2,1)S(1)}, u32[]{:S(2)}, u32[]{:S(2)}) collective-permute-start(bf16[128,512]{1,0:T(8,128)(2,1)S(1)} %get-tuple-element.65), channel_id=1, source_target_pairs={{0,4},{4,0},{1,5},{5,1},{2,6},{6,2},{3,7},{7,3},{8,12},{12,8},{9,1... | collective-permute-start | bytes 393224 | tf_op jit(solution)/shard_map/ppermute | solution.py:504
  67.8 8.0 %copy-start = (f32[1024]{0:T(1024)S(1)}, f32[1024]{0:T(1024)}, u32[]{:S(2)}) copy-start(f32[1024]{0:T(1024)} %param.17) | copy-start | bytes 12292

commit v2 on v1

--- a/solution.py
+++ b/solution.py
@@ -132,7 +132,7 @@
 
 def state_kernel(*refs):
     inputs, rest = refs[:7], refs[18:]
-    outputs, (xm_ref, pm_ref, sums_ref, send_ref), scratch = rest[:11], rest[11:15], rest[15:]
+    outputs, (xm_ref, pm_ref, sums_ref), scratch = rest[:11], rest[11:14], rest[14:]
     factor_ref = outputs[3]
     near_x, near_proj, to_end_ref, end_ref, tapx_ref, tapp_ref = outputs[5:11]
     core = lax.axis_index("core")
@@ -168,7 +168,6 @@
         )
         sums_ref[half, STATE + 24 :, : 2 * STATE] = jnp.where(is_first, tail_proj, head_proj)
         sums_ref[half, STATE + 24 :, 2 * STATE :] = jnp.zeros((8, HALF - 2 * STATE), F32)
-    send_ref[...] = sums_ref[1 - core]
 
 
 def first_of(halo_x, halo_proj, head_x, head_proj, tapx, tapp, ext_ref, extp_ref):
@@ -186,23 +185,26 @@
 
 
 def first_kernel(
-    halo_ref, x_ref, proj_ref, end_ref, tapx_ref, tapp_ref, own_ref, send_ref, ext_ref, extp_ref
+    halo_ref, x_ref, proj_ref, end_ref, tapx_ref, tapp_ref, before_ref, sums_ref, send_ref,
+    ext_ref, extp_ref,
 ):
+    core = lax.axis_index("core")
     halo = halo_ref[...].astype(F32)
     xm, pm = first_of(
         halo[:, :CHANNELS], halo[:, CHANNELS:], x_ref[:8].astype(F32), proj_ref[:8].astype(F32),
         tapx_ref[...], tapp_ref[...], ext_ref, extp_ref,
     )
-    weighted = (xm.astype(F32) * end_ref[...]).astype(BF16)
-    own_ref[:, :HALF] = weighted[:, :HALF]
-    own_ref[:, HALF:] = pm[:, :STATE]
-    send_ref[:, :HALF] = weighted[:, HALF:]
-    send_ref[:, HALF:] = pm[:, :STATE]
+    end = jnp.where(first_core(), end_ref[...], 0.0)
+    added = dot(pm[:, :STATE], (xm.astype(F32) * end).astype(BF16), ((0,), (0,)))
+    for half in range(2):
+        at = slice(half * HALF, (half + 1) * HALF)
+        sums_ref[half, :STATE] = before_ref[half, :STATE] + added[:, at]
+    send_ref[...] = sums_ref[1 - core]
 
 
 def join_kernel(
-    sums_ref, recv_ref, x_ref, proj_ref, tapx_ref, tapp_ref, own_rows_ref, recv_rows_ref,
-    message_ref, first_ref, ext_ref, extp_ref,
+    sums_ref, recv_ref, x_ref, proj_ref, tapx_ref, tapp_ref, message_ref, first_ref, ext_ref,
+    extp_ref,
 ):
     core = lax.axis_index("core")
     is_first = first_core()
@@ -223,17 +225,11 @@
     )
     end = jnp.where(is_first, other[STATE + 16 : STATE + 24], own[STATE + 16 : STATE + 24])
     added = dot(pm[:, :STATE], (xm.astype(F32) * end).astype(BF16), ((0,), (0,)))
-    rows = jnp.where(
-        is_first, own_rows_ref[...].astype(F32), recv_rows_ref[...].astype(F32)
-    ).astype(BF16)
-    added_first = dot(rows[:, HALF:], rows[:, :HALF], ((0,), (0,)))
     first = jnp.where(is_first, own[: STATE + 8], other[: STATE + 8])
     second = jnp.where(is_first, other[: STATE + 8], own[: STATE + 8])
-    first_state = first[:STATE] + added_first
-    first_ref[:STATE] = first_state
-    first_ref[STATE:] = first[STATE:]
+    first_ref[...] = first
     factor = second[STATE:] * first[STATE:]
-    total = second[STATE : STATE + 1] * first_state + (second[:STATE] + added)
+    total = second[STATE : STATE + 1] * first[:STATE] + (second[:STATE] + added)
     high = factor.astype(BF16)
     low = (factor - high.astype(F32)).astype(BF16)
     row = lax.broadcasted_iota(jnp.int32, (8, HALF), 0)
@@ -464,7 +460,7 @@
     halo = lax.ppermute(tail, ("y", "z", "core"), [(i, i + 1) for i in range(1, 2 * CHIPS - 1, 2)])
     (
         step, log_rows, log_columns, _, now, near_x, near_proj, _, end, tapx, tapp,
-        xm, pm, sums, send,
+        xm, pm, before,
     ) = call(
         state_kernel,
         prepared
@@ -472,28 +468,29 @@
             shape(whole, BF16),
             shape((TOKENS_LOCAL, 2 * STATE), BF16),
             shape((2, rows, HALF), F32),
-            shape((rows, HALF), F32),
         ),
         loads,
         10**9,
         in_specs=[ANY] * 7 + [NEAR] * 11,
         input_output_aliases={7 + i: i for i in range(11)},
     )(*sources, *(near(value) for value in early))
+    small = [pltpu.VMEM((16, CHANNELS), F32), pltpu.VMEM((16, 2 * STATE), F32)]
+    sums, send = call(
+        first_kernel,
+        (shape((2, rows, HALF), F32), shape((rows, HALF), F32)),
+        small,
+        input_output_aliases={6: 0},
+    )(
+        near(halo), near(near_x), near(near_proj), near(end), near(tapx), near(tapp), near(before)
+    )
     swap = [(0, 1), (1, 0)]
     other = lax.ppermute(send, "core", swap)
-    small = [pltpu.VMEM((16, CHANNELS), F32), pltpu.VMEM((16, 2 * STATE), F32)]
-    ranks = shape((8, HALF + STATE), BF16)
-    own_rows, rows_send = call(first_kernel, (ranks, ranks), small)(
-        near(halo), near(near_x), near(near_proj), near(end), near(tapx), near(tapp)
-    )
-    came_rows = lax.ppermute(rows_send, "core", [(0, 1)])
     message, first = call(
         join_kernel,
         (shape((CHIPS, 5, 2, 128), BF16), shape((STATE + 8, HALF), F32)),
         [pltpu.VMEM((16, HALF), F32), pltpu.VMEM((16, 2 * STATE), F32)],
     )(
         near(sums), near(other), near(near_x), near(near_proj), near(tapx), near(tapp),
-        near(own_rows), near(came_rows),
     )
     gathered = lax.all_to_all(message, chips, 0, 0, tiled=True)
     entering = call(scan_kernel, shape((CHIPS, 8, 2, 128), BF16))(near(gathered))

time: 77.1 us -> 73.7 us (0.956)
  starting transfers between devices: 16.7 us -> 14.8 us
  waiting for transfers between devices: 2.66 us -> 1.24 us
    ppermute x1, starting transfers between devices: 8.74 us -> 5.57 us  [shards(): other = lax.ppermute(send, 'core', swap)]
    ppermute x1, starting transfers between devices: 1.29 us -> 3.85 us  [shards(): lax.ppermute(tail, ('y', 'z', 'core'), [(i, i + 1) for i in range(1, 2 *...]
    ppermute x1 -> x0, waiting for transfers between devices: 1.77 us -> none  [shards(): came_rows = lax.ppermute(rows_send, 'core', [(0, 1)])]
    ppermute x1 -> x0, starting transfers between devices: 1.29 us -> none  [shards(): came_rows = lax.ppermute(rows_send, 'core', [(0, 1)])]
    ppermute x1, waiting for transfers between devices: 0.01 us -> 1.23 us  [shards(): other = lax.ppermute(send, 'core', swap)]
    ppermute x1, waiting for transfers between devices: 0.89 us -> 0.01 us  [shards(): lax.ppermute(tail, ('y', 'z', 'core'), [(i, i + 1) for i in range(1, 2 *...]
  transfers between devices with their start and end apart: 4 -> 3, of which waited for: 2 -> 1; matrix products, arithmetic and copies ran while one was open for 0% -> 0% of each run, Pallas kernels for 2% -> 4%
where the time goes in v2:
time: 73.7 us; the launch traced here: 73.4 us
  blocking collectives  50.5 us (69%)
  starting transfers between devices  14.8 us (20%)
  Pallas kernels  6.72 us (9%)
  waiting for transfers between devices  1.24 us (2%)
    all_to_all x1, blocking collectives, shards(): gathered = lax.all_to_all(message, chips, 0, 0, tiled=True)  25.2 us
    all_to_all x1, blocking collectives, shards(): returned = lax.all_to_all(entering, chips, 0, 0, tiled=True)  17.3 us
    all_to_all x1, blocking collectives, shards(): squares = lax.all_to_all(square, 'head', 0, 0, tiled=True)  8.02 us
    ppermute x1, starting transfers between devices, shards(): other = lax.ppermute(send, 'core', swap)  5.57 us
    ppermute x1, starting transfers between devices, shards(): got = lax.ppermute(give, 'core', swap)  5.38 us
    ppermute x1, starting transfers between devices, shards(): lax.ppermute(tail, ('y', 'z', 'core'), [(i, i + 1) for i in range(1, 2 *...  3.85 us
    pallas_call x1, Pallas kernels, shards(): call(early_kernel, (shape((8, CHANNELS + 2 * STATE), BF16),) + prepared,...  1.61 us
  transfers between devices with their start and end apart: 3, of which 1 were waited for; matrix products, arithmetic and copies ran while one was open for 0% of the time, Pallas kernels for 4%

profile of v2, /device:TPU:1, one launch (start us, length us, event | category | flops | bytes accessed | tf_op | source)
XLA Modules:
  0.0 73.4 jit_solution(1139103895817205719)
XLA Ops:
  0.0 1.6 %shard_map.91 = (bf16[8,1280]{1,0:T(8,128)(2,1)S(1)}, f32[16,256]{1,0:T(8,128)S(1)}, f32[16,256]{1,0:T(8,128)S(1)}, f32[256,128]{1,0:T(8,128)S(1)}, f32[8,1024]{...) custom-call(bf16[256,1024]{1,0:T(8,128)(2,1)} %bitcast.12, ...), custom_call_target="tpu_custom_call" | custom-call | tf_op jit(solution)/shard_map/pallas_call | solution.py:454
  1.6 3.8 %collective-permute-start = (bf16[8,1280]{1,0:T(8,128)(2,1)S(1)}, bf16[8,1280]{1,0:T(8,128)(2,1)S(1)}, u32[]{:S(2)}, u32[]{:S(2)}) collective-permute-start(bf16[8,1280]{1,0:T(8,128)(2,1)S(1)} %get-tuple-element.40), channel_id=1, source_target_pairs={{4,8},{12,16},{20,24},{28,32},{36,40},{44,48},{52,56},{60,64},{68,... | collective-permute-start | bytes 61448 | tf_op jit(solution)/shard_map/ppermute | solution.py:460
  5.5 1.3 %shard_map.92 = (f32[16,256]{1,0:T(8,128)S(1)}, f32[16,256]{1,0:T(8,128)S(1)}, f32[256,128]{1,0:T(8,128)S(1)}, f32[8,1024]{1,0:T(8,128)S(1)}, f32[256,1024]{1,0:...) custom-call(bf16[256,1024]{1,0:T(8,128)(2,1)} %bitcast.13, ...), custom_call_target="tpu_custom_call", output_to_operand_aliasing={{0}: (7, {}), {1}: (8, {}), {2}: (9, {}), {3}: (10, {}), {4... | custom-call | flops 1000000000 | tf_op jit(solution)/shard_map/pallas_call | solution.py:464
  6.8 0.0 collective-permute-done.halo_ref
  6.8 0.3 shard_map.93
  7.1 5.6 %collective-permute-start.1 = (f32[160,512]{1,0:T(8,128)S(1)}, f32[160,512]{1,0:T(8,128)S(1)}, u32[]{:S(2)}, u32[]{:S(2)}) collective-permute-start(f32[160,512]{1,0:T(8,128)S(1)} %get-tuple-element.59), channel_id=1, source_target_pairs={{0,4},{4,0},{1,5},{5,1},{2,6},{6,2},{3,7},{7,3},{8,12},{12,8},{9,1... | collective-permute-start | bytes 983048 | tf_op jit(solution)/shard_map/ppermute | solution.py:487
  12.7 1.2 %collective-permute-done.1.recv_ref = f32[160,512]{1,0:T(8,128)S(1)} collective-permute-done((f32[160,512]{1,0:T(8,128)S(1)}, f32[160,512]{1,0:T(8,128)S(1)}, u32[]{:S(2)}, u32[]{:S(2)}) %collective-permute-start.1) | collective-permute-done | bytes 327712 | tf_op jit(solution)/shard_map/ppermute | solution.py:487
  13.9 0.3 shard_map.94
  14.2 25.2 %all_to_all.15.message_ref = bf16[64,5,2,128]{3,2,1,0:T(2,128)(2,1)S(1)} all-to-all(bf16[64,5,2,128]{3,2,1,0:T(2,128)(2,1)S(1)} %get-tuple-element.60), channel_id=1, replica_groups=mesh['y'=8,'z'=8,'core'=2,'head'=4] {'y','z'}, dimensions={0} | all-to-all | bytes 327680 | tf_op jit(solution)/shard_map/all_to_all | solution.py:495
  39.5 0.3 shard_map.95
  39.8 0.0 copy-start.1
  39.8 17.3 %all_to_all.16.came_ref = bf16[64,8,2,128]{3,2,1,0:T(2,128)(2,1)S(1)} all-to-all(bf16[64,8,2,128]{3,2,1,0:T(2,128)(2,1)S(1)} %shard_map.95), channel_id=1, replica_groups=mesh['y'=8,'z'=8,'core'=2,'head'=4] {'y','z'}, dimensions={0} | all-to-all | bytes 524288 | tf_op jit(solution)/shard_map/all_to_all | solution.py:497
  57.0 0.2 shard_map.96
  57.3 5.4 %collective-permute-start.2 = (bf16[128,512]{1,0:T(8,128)(2,1)S(1)}, bf16[128,512]{1,0:T(8,128)(2,1)S(1)}, u32[]{:S(2)}, u32[]{:S(2)}) collective-permute-start(bf16[128,512]{1,0:T(8,128)(2,1)S(1)} %get-tuple-element.63), channel_id=1, source_target_pairs={{0,4},{4,0},{1,5},{5,1},{2,6},{6,2},{3,7},{7,3},{8,12},{12,8},{9,1... | collective-permute-start | bytes 393224 | tf_op jit(solution)/shard_map/ppermute | solution.py:501
  62.7 0.0 copy-done.1
  62.7 1.3 %shard_map.97 = (f32[256,1024]{1,0:T(8,128)S(1)}, bf16[256,128]{1,0:T(8,128)(2,1)S(1)}, f32[256,1024]{1,0:T(8,128)S(1)}) custom-call(bf16[256,1024]{1,0:T(8,128)(2,1)S(1)} %get-tuple-element.64.early_ref, bf16[256,256]{1,0:T(8,128)(2,1)S(1)} %get-tuple-element.65.pm_ref, f32[16,256]{1,0:T(8,128)S(1)} %get-tuple-element.66.step_rows, ...), custom_call_target="tpu_custom_call" | custom-call | flops 10000000000 | tf_op jit(solution)/shard_map/pallas_call | solution.py:502
  64.0 0.0 collective-permute-done.2.recv_ref
  64.0 0.4 shard_map.98
  64.4 0.0 copy-start
  64.4 8.0 %all_to_all.17.square_ref = f32[4,8,128]{2,1,0:T(8,128)S(1)} all-to-all(f32[4,8,128]{2,1,0:T(8,128)S(1)} %get-tuple-element.74), channel_id=1, replica_groups=mesh['y'=8,'z'=8,'core'=2,'head'=4] {'head'}, dimensions={0} | all-to-all | bytes 32768 | tf_op jit(solution)/shard_map/all_to_all | solution.py:515
  72.4 0.0 copy-done
  72.4 1.0 %shard_map.99 = bf16[256,1024]{1,0:T(8,128)(2,1)} custom-call(f32[256,1024]{1,0:T(8,128)S(1)} %get-tuple-element.73.gated_ref, f32[4,8,128]{2,1,0:T(8,128)S(1)} %all_to_all.17.square_ref, f32[1,1024]{1,0:T(1,128)S(1)} %bitcast.10), custom_call_target="tpu_custom_call" | custom-call | tf_op jit(solution)/shard_map/pallas_call | solution.py:516
Async XLA Ops:
  1.6 5.2 %collective-permute-start = (bf16[8,1280]{1,0:T(8,128)(2,1)S(1)}, bf16[8,1280]{1,0:T(8,128)(2,1)S(1)}, u32[]{:S(2)}, u32[]{:S(2)}) collective-permute-start(bf16[8,1280]{1,0:T(8,128)(2,1)S(1)} %get-tuple-element.40), channel_id=1, source_target_pairs={{4,8},{12,16},{20,24},{28,32},{36,40},{44,48},{52,56},{60,64},{68,... | collective-permute-start | bytes 61448 | tf_op jit(solution)/shard_map/ppermute | solution.py:460
  7.1 6.8 %collective-permute-start.1 = (f32[160,512]{1,0:T(8,128)S(1)}, f32[160,512]{1,0:T(8,128)S(1)}, u32[]{:S(2)}, u32[]{:S(2)}) collective-permute-start(f32[160,512]{1,0:T(8,128)S(1)} %get-tuple-element.59), channel_id=1, source_target_pairs={{0,4},{4,0},{1,5},{5,1},{2,6},{6,2},{3,7},{7,3},{8,12},{12,8},{9,1... | collective-permute-start | bytes 983048 | tf_op jit(solution)/shard_map/ppermute | solution.py:487
  39.8 22.9 %copy-start.1 = (bf16[1,256,1024]{2,1,0:T(8,128)(2,1)S(1)}, bf16[1,256,1024]{2,1,0:T(8,128)(2,1)}, u32[]{:S(2)}) copy-start(bf16[1,256,1024]{2,1,0:T(8,128)(2,1)} %param.10) | copy-start | bytes 1572868
  57.3 6.7 %collective-permute-start.2 = (bf16[128,512]{1,0:T(8,128)(2,1)S(1)}, bf16[128,512]{1,0:T(8,128)(2,1)S(1)}, u32[]{:S(2)}, u32[]{:S(2)}) collective-permute-start(bf16[128,512]{1,0:T(8,128)(2,1)S(1)} %get-tuple-element.63), channel_id=1, source_target_pairs={{0,4},{4,0},{1,5},{5,1},{2,6},{6,2},{3,7},{7,3},{8,12},{12,8},{9,1... | collective-permute-start | bytes 393224 | tf_op jit(solution)/shard_map/ppermute | solution.py:501
  64.4 8.0 %copy-start = (f32[1024]{0:T(1024)S(1)}, f32[1024]{0:T(1024)}, u32[]{:S(2)}) copy-start(f32[1024]{0:T(1024)} %param.17) | copy-start | bytes 12292

commit v3 on v1

--- a/solution.py
+++ b/solution.py
@@ -362,10 +362,8 @@
         for lane in range(HALF // 128):
             partial = partial + square[:, lane * 128 : (lane + 1) * 128]
     total = jnp.sum(jnp.transpose(partial), axis=0, keepdims=True)
-    row = lax.broadcasted_iota(jnp.int32, (8, 128), 0)
-    block = jnp.where(row == 0, total[:, :128], jnp.where(row == 1, total[:, 128:], 0.0))
-    for peer in range(4):
-        square_ref[peer] = block
+    square_ref[0:1, :] = total[:, :128]
+    square_ref[1:2, :] = total[:, 128:]
 
 
 def norm_kernel(gated_ref, square_ref, gain_ref, out_ref, near_out_ref, sems):
@@ -375,7 +373,7 @@
         [jnp.broadcast_to(scale[0:1], (128, 128)), jnp.broadcast_to(scale[1:2], (128, 128))], axis=1
     )
     column = jnp.transpose(wide)
-    chunks = 4
+    chunks = 8
     size = TOKENS_LOCAL // chunks
     copies = []
     for chunk in range(chunks):
@@ -513,13 +511,13 @@
         near(tapp),
     )
     gated, square = call(
-        gate_kernel, (shape((TOKENS_LOCAL, CHANNELS), F32), shape((4, 8, 128), F32))
+        gate_kernel, (shape((TOKENS_LOCAL, CHANNELS), F32), shape((2, 128), F32))
     )(near(keep), near(got), near(read), near(within), near(outer))
-    squares = lax.all_to_all(square, "head", 0, 0, tiled=True)
+    squares = lax.all_gather(square, "head")
     out = call(
         norm_kernel,
         pltpu.HBM((TOKENS_LOCAL, CHANNELS), BF16),
-        [pltpu.VMEM((TOKENS_LOCAL, CHANNELS), BF16), pltpu.SemaphoreType.DMA((4,))],
+        [pltpu.VMEM((TOKENS_LOCAL, CHANNELS), BF16), pltpu.SemaphoreType.DMA((8,))],
         out_specs=ANY,
     )(near(gated), near(squares), norm_gain[None])
     return out[None]

time: 77.1 us -> 76.8 us (level)
    all_to_all x1 -> x0, blocking collectives: 8.03 us -> none  [shards(): squares = lax.all_to_all(square, 'head', 0, 0, tiled=True)]
    all_gather x0 -> x1, blocking collectives: none -> 7.72 us  [shards(): squares = lax.all_gather(square, 'head')]
where the time goes in v3:
time: 76.8 us; the launch traced here: 76.5 us
  blocking collectives  50.4 us (66%)
  starting transfers between devices  16.7 us (22%)
  Pallas kernels  6.56 us (9%)
  waiting for transfers between devices  2.66 us (3%)
    all_to_all x1, blocking collectives, shards(): gathered = lax.all_to_all(message, chips, 0, 0, tiled=True)  25.5 us
    all_to_all x1, blocking collectives, shards(): returned = lax.all_to_all(entering, chips, 0, 0, tiled=True)  17.2 us
    ppermute x1, starting transfers between devices, shards(): other = lax.ppermute(send, 'core', swap)  8.74 us
    all_gather x1, blocking collectives, shards(): squares = lax.all_gather(square, 'head')  7.72 us
    ppermute x1, starting transfers between devices, shards(): got = lax.ppermute(give, 'core', swap)  5.38 us
    ppermute x1, waiting for transfers between devices, shards(): came_rows = lax.ppermute(rows_send, 'core', [(0, 1)])  1.77 us
    pallas_call x1, Pallas kernels, shards(): call(early_kernel, (shape((8, CHANNELS + 2 * STATE), BF16),) + prepared,...  1.61 us
  transfers between devices with their start and end apart: 4, of which 2 were waited for; matrix products, arithmetic and copies ran while one was open for 0% of the time, Pallas kernels for 2%

profile of v3, /device:TPU:1, one launch (start us, length us, event | category | flops | bytes accessed | tf_op | source)
XLA Modules:
  0.0 76.5 jit_solution(15129269496794188667)
XLA Ops:
  0.0 1.6 %shard_map.91 = (bf16[8,1280]{1,0:T(8,128)(2,1)S(1)}, f32[16,256]{1,0:T(8,128)S(1)}, f32[16,256]{1,0:T(8,128)S(1)}, f32[256,128]{1,0:T(8,128)S(1)}, f32[8,1024]{...) custom-call(bf16[256,1024]{1,0:T(8,128)(2,1)} %bitcast.14, ...), custom_call_target="tpu_custom_call" | custom-call | tf_op jit(solution)/shard_map/pallas_call | solution.py:456
  1.6 1.3 %shard_map.92 = (f32[16,256]{1,0:T(8,128)S(1)}, f32[16,256]{1,0:T(8,128)S(1)}, f32[256,128]{1,0:T(8,128)S(1)}, f32[8,1024]{1,0:T(8,128)S(1)}, f32[256,1024]{1,0:...) custom-call(bf16[256,1024]{1,0:T(8,128)(2,1)} %bitcast.15, ...), custom_call_target="tpu_custom_call", output_to_operand_aliasing={{0}: (7, {}), {1}: (8, {}), {2}: (9, {}), {3}: (10, {}), {4... | custom-call | flops 1000000000 | tf_op jit(solution)/shard_map/pallas_call | solution.py:466
  3.0 8.7 %collective-permute-start = (f32[160,512]{1,0:T(8,128)S(1)}, f32[160,512]{1,0:T(8,128)S(1)}, u32[]{:S(2)}, u32[]{:S(2)}) collective-permute-start(f32[160,512]{1,0:T(8,128)S(1)} %get-tuple-element.53), channel_id=1, source_target_pairs={{0,4},{4,0},{1,5},{5,1},{2,6},{6,2},{3,7},{7,3},{8,12},{12,8},{9,1... | collective-permute-start | bytes 983048 | tf_op jit(solution)/shard_map/ppermute | solution.py:481
  11.7 1.3 %collective-permute-start.1 = (bf16[8,1280]{1,0:T(8,128)(2,1)S(1)}, bf16[8,1280]{1,0:T(8,128)(2,1)S(1)}, u32[]{:S(2)}, u32[]{:S(2)}) collective-permute-start(bf16[8,1280]{1,0:T(8,128)(2,1)S(1)} %get-tuple-element.58), channel_id=1, source_target_pairs={{4,8},{12,16},{20,24},{28,32},{36,40},{44,48},{52,56},{60,64},{68,... | collective-permute-start | bytes 61448 | tf_op jit(solution)/shard_map/ppermute | solution.py:462
  13.0 0.9 %collective-permute-done.1.halo_ref = bf16[8,1280]{1,0:T(8,128)(2,1)S(1)} collective-permute-done((bf16[8,1280]{1,0:T(8,128)(2,1)S(1)}, bf16[8,1280]{1,0:T(8,128)(2,1)S(1)}, u32[]{:S(2)}, u32[]{:S(2)}) %collective-permute-start.1) | collective-permute-done | bytes 20512 | tf_op jit(solution)/shard_map/ppermute | solution.py:462
  13.9 0.1 shard_map.93
  14.0 1.3 %collective-permute-start.2 = (bf16[8,640]{1,0:T(8,128)(2,1)S(1)}, bf16[8,640]{1,0:T(8,128)(2,1)S(1)}, u32[]{:S(2)}, u32[]{:S(2)}) collective-permute-start(bf16[8,640]{1,0:T(8,128)(2,1)S(1)} %get-tuple-element.61), channel_id=1, source_target_pairs={{0,4},{1,5},{2,6},{3,7},{8,12},{9,13},{10,14},{11,15},{16,20},{17,... | collective-permute-start | bytes 30728 | tf_op jit(solution)/shard_map/ppermute | solution.py:487
  15.3 1.8 %collective-permute-done.2.recv_rows_ref = bf16[8,640]{1,0:T(8,128)(2,1)S(1)} collective-permute-done((bf16[8,640]{1,0:T(8,128)(2,1)S(1)}, bf16[8,640]{1,0:T(8,128)(2,1)S(1)}, u32[]{:S(2)}, u32[]{:S(2)}) %collective-permute-start.2) | collective-permute-done | bytes 10272 | tf_op jit(solution)/shard_map/ppermute | solution.py:487
  17.0 0.0 collective-permute-done.recv_ref
  17.0 0.4 shard_map.94
  17.4 25.5 %all_to_all.10.message_ref = bf16[64,5,2,128]{3,2,1,0:T(2,128)(2,1)S(1)} all-to-all(bf16[64,5,2,128]{3,2,1,0:T(2,128)(2,1)S(1)} %get-tuple-element.62), channel_id=1, replica_groups=mesh['y'=8,'z'=8,'core'=2,'head'=4] {'y','z'}, dimensions={0} | all-to-all | bytes 327680 | tf_op jit(solution)/shard_map/all_to_all | solution.py:496
  42.9 0.3 shard_map.95
  43.2 0.0 copy-start.1
  43.2 17.2 %all_to_all.11.came_ref = bf16[64,8,2,128]{3,2,1,0:T(2,128)(2,1)S(1)} all-to-all(bf16[64,8,2,128]{3,2,1,0:T(2,128)(2,1)S(1)} %shard_map.95), channel_id=1, replica_groups=mesh['y'=8,'z'=8,'core'=2,'head'=4] {'y','z'}, dimensions={0} | all-to-all | bytes 524288 | tf_op jit(solution)/shard_map/all_to_all | solution.py:498
  60.4 0.2 shard_map.96
  60.7 5.4 %collective-permute-start.3 = (bf16[128,512]{1,0:T(8,128)(2,1)S(1)}, bf16[128,512]{1,0:T(8,128)(2,1)S(1)}, u32[]{:S(2)}, u32[]{:S(2)}) collective-permute-start(bf16[128,512]{1,0:T(8,128)(2,1)S(1)} %get-tuple-element.65), channel_id=1, source_target_pairs={{0,4},{4,0},{1,5},{5,1},{2,6},{6,2},{3,7},{7,3},{8,12},{12,8},{9,1... | collective-permute-start | bytes 393224 | tf_op jit(solution)/shard_map/ppermute | solution.py:502
  66.1 0.0 copy-done.1
  66.1 1.3 %shard_map.97 = (f32[256,1024]{1,0:T(8,128)S(1)}, bf16[256,128]{1,0:T(8,128)(2,1)S(1)}, f32[256,1024]{1,0:T(8,128)S(1)}) custom-call(bf16[256,1024]{1,0:T(8,128)(2,1)S(1)} %get-tuple-element.66.early_ref, bf16[256,256]{1,0:T(8,128)(2,1)S(1)} %get-tuple-element.67.pm_ref, f32[16,256]{1,0:T(8,128)S(1)} %get-tuple-element.68.step_rows, ...), custom_call_target="tpu_custom_call" | custom-call | flops 10000000000 | tf_op jit(solution)/shard_map/pallas_call | solution.py:503
  67.4 0.0 collective-permute-done.3.recv_ref
  67.4 0.4 shard_map.98
  67.8 0.0 copy-start
  67.8 7.7 %all-gather.1.square_ref = f32[4,2,128]{2,1,0:T(2,128)S(1)} all-gather(f32[1,2,128]{2,1,0:T(2,128)S(1)} %bitcast.12), channel_id=2, replica_groups=mesh['y'=8,'z'=8,'core'=2,'head'=4] {'head'}, dimensions={0}, use_global_device_ids=true | all-gather | bytes 5120 | tf_op jit(solution)/shard_map/all_gather | solution.py:516
  75.5 0.0 copy-done
  75.5 1.0 %shard_map.99 = bf16[256,1024]{1,0:T(8,128)(2,1)} custom-call(f32[256,1024]{1,0:T(8,128)S(1)} %get-tuple-element.75.gated_ref, f32[4,2,128]{2,1,0:T(2,128)S(1)} %all-gather.1.square_ref, f32[1,1024]{1,0:T(1,128)S(1)} %bitcast.11), custom_call_target="tpu_custom_call" | custom-call | tf_op jit(solution)/shard_map/pallas_call | solution.py:517
Async XLA Ops:
  3.0 14.1 %collective-permute-start = (f32[160,512]{1,0:T(8,128)S(1)}, f32[160,512]{1,0:T(8,128)S(1)}, u32[]{:S(2)}, u32[]{:S(2)}) collective-permute-start(f32[160,512]{1,0:T(8,128)S(1)} %get-tuple-element.53), channel_id=1, source_target_pairs={{0,4},{4,0},{1,5},{5,1},{2,6},{6,2},{3,7},{7,3},{8,12},{12,8},{9,1... | collective-permute-start | bytes 983048 | tf_op jit(solution)/shard_map/ppermute | solution.py:481
  11.7 2.2 %collective-permute-start.1 = (bf16[8,1280]{1,0:T(8,128)(2,1)S(1)}, bf16[8,1280]{1,0:T(8,128)(2,1)S(1)}, u32[]{:S(2)}, u32[]{:S(2)}) collective-permute-start(bf16[8,1280]{1,0:T(8,128)(2,1)S(1)} %get-tuple-element.58), channel_id=1, source_target_pairs={{4,8},{12,16},{20,24},{28,32},{36,40},{44,48},{52,56},{60,64},{68,... | collective-permute-start | bytes 61448 | tf_op jit(solution)/shard_map/ppermute | solution.py:462
  14.0 3.1 %collective-permute-start.2 = (bf16[8,640]{1,0:T(8,128)(2,1)S(1)}, bf16[8,640]{1,0:T(8,128)(2,1)S(1)}, u32[]{:S(2)}, u32[]{:S(2)}) collective-permute-start(bf16[8,640]{1,0:T(8,128)(2,1)S(1)} %get-tuple-element.61), channel_id=1, source_target_pairs={{0,4},{1,5},{2,6},{3,7},{8,12},{9,13},{10,14},{11,15},{16,20},{17,... | collective-permute-start | bytes 30728 | tf_op jit(solution)/shard_map/ppermute | solution.py:487
  43.2 22.9 %copy-start.1 = (bf16[1,256,1024]{2,1,0:T(8,128)(2,1)S(1)}, bf16[1,256,1024]{2,1,0:T(8,128)(2,1)}, u32[]{:S(2)}) copy-start(bf16[1,256,1024]{2,1,0:T(8,128)(2,1)} %param.10) | copy-start | bytes 1572868
  60.7 6.7 %collective-permute-start.3 = (bf16[128,512]{1,0:T(8,128)(2,1)S(1)}, bf16[128,512]{1,0:T(8,128)(2,1)S(1)}, u32[]{:S(2)}, u32[]{:S(2)}) collective-permute-start(bf16[128,512]{1,0:T(8,128)(2,1)S(1)} %get-tuple-element.65), channel_id=1, source_target_pairs={{0,4},{4,0},{1,5},{5,1},{2,6},{6,2},{3,7},{7,3},{8,12},{12,8},{9,1... | collective-permute-start | bytes 393224 | tf_op jit(solution)/shard_map/ppermute | solution.py:502
  67.8 7.7 %copy-start = (f32[1024]{0:T(1024)S(1)}, f32[1024]{0:T(1024)}, u32[]{:S(2)}) copy-start(f32[1024]{0:T(1024)} %param.17) | copy-start | bytes 12292
